TPU v7x, 512 devices: a 4x2x32 block of a 4x8x32 slice. The times are simulated.
512 devices in a mesh: groups: 2 (over y), pix: 32 (over z), sub: 4 (over x), rep: 2 (over core).
Axes of the slice: x: 4, y: 2, z: 32, core: 2. Of those that a mesh axis runs over, the one named last changes fastest.
The devices are a block of a 4x8x32 slice.
Arguments:
- gaia_pos: float32 [2, 65536], P(None, ('groups', 'pix', 'sub', 'rep')), parts along dimension 1, may hold values from 0 to 1
- gaia_shape: float32 [2, 65536], P(None, ('groups', 'pix', 'sub', 'rep')), parts along dimension 1, may hold values from 0.15 to 0.6
- gaia_corr: float32 [65536], P(('groups', 'pix', 'sub', 'rep')), parts along dimension 0, may hold values from -0.8 to 0.8
- gaia_dest: int32 [65536, 1], P(('groups', 'pix', 'sub', 'rep')), parts along dimension 0, may hold values from 0 to 127; in each aligned block of 128 rows (0 to 127, 128 to 255, ...) at most 2 rows name the same one
- gaia_cell: int32 [65536], P(('groups', 'pix', 'sub', 'rep')), parts along dimension 0, may hold values from 0 to 127
- wise_pos: float32 [2, 65536], P(None, ('groups', 'pix', 'sub', 'rep')), parts along dimension 1, may hold values from 0 to 1
- wise_shape: float32 [2, 65536], P(None, ('groups', 'pix', 'sub', 'rep')), parts along dimension 1, may hold values from 0.15 to 0.6
- wise_corr: float32 [65536], P(('groups', 'pix', 'sub', 'rep')), parts along dimension 0, may hold values from -0.8 to 0.8
- wise_dest: int32 [65536, 1], P(('groups', 'pix', 'sub', 'rep')), parts along dimension 0, may hold values from 0 to 127; in each aligned block of 128 rows (0 to 127, 128 to 255, ...) at most 2 rows name the same one
- wise_cell: int32 [65536], P(('groups', 'pix', 'sub', 'rep')), parts along dimension 0, may hold values from 0 to 127
Outputs:
- gaia_like: float32 [65536], P(('groups', 'pix', 'sub', 'rep')), parts along dimension 0
- gaia_offset: float32 [2, 65536], P(None, ('groups', 'pix', 'sub', 'rep')), parts along dimension 1
- wise_like: float32 [65536], P(('groups', 'pix', 'sub', 'rep')), parts along dimension 0
There are 2 independent parts, one for each index of `groups`. A program takes and returns all parts, laid end to end along the dimension named above; each array names one. Nothing has to cross between parts.
Inputs may be any that keep to these rules, and one draw needn't show every extreme that they name: `gaia_dest`: among the 128 sources of one device no target appears more than 2 times, and some target appears exactly 2 times; the owner of a source is dest // 4. `wise_dest`: among the 128 sources of one device no target appears more than 2 times, and some target appears exactly 2 times; the owner of a source is dest // 4. `gaia_cell`: pixel row inside the band is cell // 64, column cell % 64. `wise_cell`: pixel row inside the band is cell // 64, column cell % 64.
All inputs are finite; a program needn't handle non-finite values.
Results may differ from a plain program's by a relative error of at most 0.0003.
Values sent between devices are 32-bit elements; how exact they have to be, the bound alone decides.
No kernel may reach another device: no remote copies, remote signals or barrier semaphores. Data moves between devices by JAX's collectives and lax.ppermute only.
A program may use at most 64 MiB of HBM per device.

v0:
```python
import math

import jax
import jax.numpy as jnp
from jax import lax
from jax.experimental import pallas as pl
from jax.experimental.pallas import tpu as pltpu
from jax.sharding import PartitionSpec as P

NCOL = 64
CAP = 2
LANES = 128
SLOT_LANES = 16
FIELDS = 8
EMPTY_BIT = 4096
ROW_BIT = 8192
LAMBDA = 2.0 * math.log(2.0)
GAIN = LAMBDA / (2.0 * math.pi)
GROUPS = 8
USED = 6
PART = 3
INTERPRET = False

f32 = jnp.float32
bf16 = jnp.bfloat16
i32 = jnp.int32


def iota(shape, dim):
    return lax.broadcasted_iota(i32, shape, dim)


def split3(x):
    high = x.astype(bf16)
    rest = x - high.astype(f32)
    middle = rest.astype(bf16)
    low = (rest - middle.astype(f32)).astype(bf16)
    return high, middle, low


def dot(a, b, contract):
    return lax.dot_general(a, b, (contract, ((), ())), preferred_element_type=f32)


def one_hot(mask):
    return jnp.where(mask, 1.0, 0.0).astype(bf16)


def call(body, outs, scratch=(), grant=8 << 20, **more):
    return pl.pallas_call(
        body,
        out_shape=outs,
        **more,
        scratch_shapes=list(scratch),
        compiler_params=pltpu.CompilerParams(vmem_limit_bytes=grant),
        interpret=INTERPRET,
    )


def ring_start(pix_count):
    return pix_count * 3 // 4


def part_rows():
    return -(-(PART * 2 * USED + 2) // 8) * 8


def tile_row(t, c):
    return t // PART * part_rows() + t % PART * 2 * USED + c * USED


def owners_and_ranks(dest_g, dest_w, sub_count):
    n = dest_g.shape[1]
    shift = sub_count.bit_length() - 1
    own_g, own_w = dest_g >> shift, dest_w >> shift
    both = jnp.concatenate([own_g.astype(f32), own_w.astype(f32), jnp.zeros((6, n), f32)], axis=0)
    columns = jnp.transpose(both)
    earlier = iota((n, n), 0) < iota((n, n), 1)

    def rank(row, column):
        same = (row.astype(f32) == column) & earlier
        return jnp.sum(jnp.where(same, 1.0, 0.0), axis=0, keepdims=True).astype(i32)

    return own_g, own_w, rank(own_g, columns[:, 0:1]), rank(own_w, columns[:, 1:2])


def send_body(pix_count, sub_count, peers):
    slots = CAP * sub_count
    turn = pix_count - ring_start(pix_count)

    def body(*refs):
        gp, gs, gc, gd, gl, wp, ws, wc, wd, wl, msg, places = refs
        n = gp.shape[1]
        own_g, own_w, rank_g, rank_w = owners_and_ranks(gd[...], wd[...], sub_count)

        def fields(pos, shape, corr, cell):
            a, b = shape[0:1, :], shape[1:2, :]
            return jnp.concatenate(
                [
                    pos[0:1, :],
                    pos[1:2, :],
                    (a * a) * LAMBDA,
                    (b * b) * LAMBDA,
                    ((corr * a) * b) * (2.0 * LAMBDA),
                    cell.astype(f32) + 1.0,
                    jnp.zeros((2, n), f32),
                ],
                axis=0,
            )

        data_g = fields(gp, gs, gc[...], gl[...])
        data_w = fields(wp, ws, wc[...], wl[...])
        zero = jnp.zeros((FIELDS, n), f32)
        left, right = [], []
        for s in range(slots):
            left += [jnp.where(rank_g == s, data_g, 0.0), zero]
            right += [zero, jnp.where(rank_w == s, data_w, 0.0)]
        table = jnp.concatenate([jnp.concatenate(left, axis=0), jnp.concatenate(right, axis=0)], axis=1)
        rows = 3 * peers
        r = iota((rows, 2 * n), 0)
        peer = jnp.floor((r.astype(f32) + 0.5) * (1.0 / 3.0)).astype(i32)
        side = r - 3 * peer
        band = (peer - turn) & (peers - 1)
        owner = jnp.concatenate([own_g, own_w], axis=1)
        upper = jnp.concatenate([gl[...], wl[...]], axis=1) >> (NCOL.bit_length() - 1)
        edge = (side == 1) | (upper == jnp.where(side == 0, 1, 0))
        pick = one_hot((owner == band + side - 1) & (band < pix_count) & edge)
        msg[...] = sum(dot(pick, part, ((1,), (1,))) for part in split3(table))
        at = [(o + turn) & (peers - 1) for o in (own_g, own_w)]
        places[...] = jnp.concatenate(at + [rank_g, rank_w, jnp.zeros((4, n), i32)], axis=0)

    return body


def compact_body(peers, slots, members, width):
    lanes = -(-3 * peers // LANES) * LANES
    tiles = width // LANES

    def body(got, out, rest, own, ranks, chunk):
        parts = [got[pl.ds(j, peers, stride=3), :] for j in (1, 0, 2)]
        parts.append(jnp.zeros((lanes - 3 * peers, LANES), f32))
        data = jnp.transpose(jnp.concatenate(parts, axis=0))
        lane8 = iota((FIELDS, lanes), 1)
        row8 = iota((FIELDS, lanes), 0)
        row_of = iota((FIELDS, LANES), 0)
        is_own = lane8 < peers
        is_low = (lane8 >= peers) & (lane8 < 2 * peers)
        before = one_hot(iota((lanes, lanes), 0) < iota((lanes, lanes), 1))
        below = one_hot(iota((slots, slots), 1) < iota((slots, slots), 0))
        goal = iota((LANES, lanes), 0).astype(f32)
        chunk[...] = jnp.zeros(chunk.shape, f32)
        own[...] = jnp.zeros(own.shape, f32)
        rank_rows, ready = [], []
        for c in range(2):
            pieces, codes = [], []
            for s in range(slots):
                x = data[s * SLOT_LANES + c * FIELDS : s * SLOT_LANES + (c + 1) * FIELDS, :]
                code = x[5:6, :]
                filled = code > 0.5
                cell = code.astype(i32) - 1
                row = jnp.where(is_own, cell >> 6, jnp.where(is_low, -1, 2)).astype(f32)
                away = jnp.where(is_own, 0, jnp.where(is_low, 512, 256))
                own_row = jnp.where(is_own, (cell >> 6) * ROW_BIT, 0)
                seen = ((cell & (NCOL - 1)) - away + EMPTY_BIT + own_row).astype(f32)
                x = jnp.where(row8 == 1, x + row, jnp.where(row8 == 5, seen, x))
                pieces.append(jnp.where(filled, x, 0.0))
                codes.append(code)
            filled = jnp.concatenate(codes, axis=0) > 0.5
            lane_s = iota((slots, lanes), 1)
            flag_own = jnp.where(filled & (lane_s < peers), 1.0, 0.0)
            flag_far = jnp.where(filled & (lane_s >= peers), 1.0, 0.0)

            def places(flag):
                inside = dot(flag.astype(bf16), before, ((1,), (0,)))
                totals = jnp.broadcast_to(jnp.sum(flag, axis=1, keepdims=True), (slots, LANES))
                ahead = dot(below, totals.astype(bf16), ((1,), (0,)))
                return inside + ahead[:, 0:1], jnp.sum(totals, axis=0, keepdims=True)

            place_own, count_own = places(flag_own)
            place_far, count_far = places(flag_far)
            place = jnp.where(flag_own > 0.5, place_own, place_far + count_own[:, 0:1])
            place = jnp.where(filled, place, -1.0)
            count = count_own + count_far
            rank_rows.append(place[:, 0:LANES])
            stacked = [jnp.concatenate(split3(p), axis=0) for p in pieces]
            total = jnp.max(count)
            chunk[PART * 2 * USED + c : PART * 2 * USED + c + 1, :] = count
            ready.append((place, stacked, count_own, total))

        def move(t, c):
            place, stacked, count_own, _ = ready[c]
            goal_t = goal + float(t * LANES)
            acc = jnp.zeros((3 * FIELDS, LANES), f32)
            for s in range(slots):
                pick = one_hot(goal_t == place[s : s + 1, :])
                acc = acc + dot(stacked[s], pick, ((1,), (1,)))
            x = acc[0:8, :] + acc[8:16, :] + acc[16:24, :]
            at = tile_row(t, c)
            chunk[at : at + USED, :] = x[0:USED, :]
            if t * LANES < own.shape[1]:
                x = jnp.where(row_of == 7, count_own, x)
                own[c * FIELDS : (c + 1) * FIELDS, t * LANES : (t + 1) * LANES] = x

        for t in range(PART):
            for c in range(2):
                move(t, c)

        @pl.when(jnp.maximum(ready[0][3], ready[1][3]) > PART * LANES)
        def _():
            for t in range(PART, tiles):
                for c in range(2):
                    move(t, c)

        ranks[...] = jnp.transpose(jnp.concatenate(rank_rows + [jnp.zeros((LANES - 2 * slots, LANES), f32)], axis=0))
        value = chunk[0 : part_rows(), :]
        for d in range(members):
            out[d] = value
        rest[...] = chunk[part_rows() :, :]

    return body


def prepare_body(peers, slots):
    used = 2 * USED

    def body(own, ranks, wide, pick):
        own_width = peers * slots
        stacked = jnp.concatenate([p.astype(f32) for p in split3(own[...])], axis=0)
        columns = jnp.transpose(stacked).astype(bf16)
        spread_to = iota((6 * FIELDS, used * LANES), 1) >> 7
        field_of = spread_to + jnp.where(spread_to >= USED, FIELDS - USED, 0)
        spread = one_hot((iota((6 * FIELDS, used * LANES), 0) & (2 * FIELDS - 1)) == field_of)
        wide[0:own_width, :] = dot(columns, spread, ((1,), (0,)))
        wide[own_width:, :] = jnp.zeros((8 * GROUPS, used * LANES), f32)
        goal = iota((peers, own_width), 1).astype(f32)
        for c in range(2):
            for s in range(slots):
                rank = ranks[0:peers, c * slots + s : c * slots + s + 1]
                pick[s * peers : (s + 1) * peers, c * own_width : (c + 1) * own_width] = one_hot(rank == goal)

    return body


def match_body(peers, slots, members, tiles):
    block = 8 * GROUPS
    whole = tiles > PART
    usual = PART
    rows = part_rows()
    own_width = peers * slots
    early = own_width * 3 // 4

    prepare = prepare_body(peers, slots)

    def body(*refs):
        near, refs = refs[: 1 + whole], refs[1 + whole :]
        own, ranks, out, refs = refs[0], refs[1], refs[2], refs[3:]
        over, refs = refs[: 1 - whole], refs[1 - whole :]
        wide, pick, line, totals, values = refs
        prepare(own, ranks, wide, pick)
        lane8 = iota((8, LANES), 1)
        count_own = [jnp.max(own[c * FIELDS + 7 : c * FIELDS + 8, 0:LANES]).astype(i32) for c in range(2)]

        def count_of(d, c):
            at = d * rows + PART * 2 * USED + c
            return jnp.max(near[0][at : at + 1, :]).astype(i32)

        counts = [[count_of(d, c) for d in range(members)] for c in range(2)]
        if not whole:
            most = counts[0][0]
            for n in counts[0][1:] + counts[1]:
                most = jnp.maximum(most, n)
            over[0][0, 0] = (most > PART * LANES).astype(i32)
            counts = [[jnp.minimum(n, PART * LANES) for n in line_counts] for line_counts in counts]
        ends = []
        for c in range(2):
            start = jnp.int32(0)
            for d in range(members):
                shift = start & (LANES - 1)
                base = start >> 7
                keep = lane8 >= shift

                def put(k, x, c=c, base=base):
                    line[c, base + k] = x

                def turned(k, c=c, d=d, shift=shift):
                    at = d * rows + tile_row(k % PART, c)
                    return pltpu.roll(near[k // PART][at : at + FIELDS, :], shift, 1)

                last = jnp.zeros((FIELDS, LANES), f32) if d == 0 else line[c, base]
                for k in range(usual):
                    now = turned(k)
                    put(k, jnp.where(keep, now, last))
                    last = now
                put(usual, jnp.where(keep, 0.0, last))
                put(usual + 1, jnp.zeros((FIELDS, LANES), f32))

                if not whole:
                    start = start + counts[c][d]
                    continue

                @pl.when(counts[c][d] > usual * LANES)
                def _(c=c, base=base, keep=keep, put=put, turned=turned):
                    last = line[c, base + usual]
                    for k in range(usual, tiles):
                        now = turned(k)
                        put(k, jnp.where(keep, now, last))
                        last = now
                    put(tiles, jnp.where(keep, 0.0, last))
                    put(tiles + 1, jnp.zeros((FIELDS, LANES), f32))

                start = start + counts[c][d]
            ends.append(lax.div(start + (2 * LANES - 1), 2 * LANES))

        for c in range(2):
            other = 1 - c
            blocks = lax.div(count_own[c] + (block - 1), block)

            def own_block(b, _, c=c, other=other):
                base = pl.multiple_of(b * block, 8)
                fields = []
                for g in range(GROUPS):
                    col = [wide[pl.ds(base + 8 * g, 8), (c * USED + f) * LANES : (c * USED + f + 1) * LANES] for f in range(USED)]
                    code = col[5].astype(i32)
                    own_code = code + (NCOL + 1 - EMPTY_BIT)
                    mask = jnp.where(code < ROW_BIT, 256, 512) | (EMPTY_BIT | (NCOL - 1))
                    fields.append((col[0] - 1.0, col[1], col[2], col[3], col[4], own_code, mask))

                def pairs(t, acc):
                    acc = [list(a) for a in acc]
                    for half in range(2):
                        at = line.at[other, 2 * t + half]
                        row = [jnp.broadcast_to(at[f : f + 1, :], (8, LANES)) for f in range(USED)]
                        code = row[5].astype(i32) - EMPTY_BIT
                        for g in range(GROUPS):
                            px, py, xx, yy, xy, own_code, mask = fields[g]
                            step = (own_code - code) & mask
                            dx = step.astype(f32) + (px - row[0])
                            dy = py - row[1]
                            sx, sy, sxy = xx + row[2], yy + row[3], xy + row[4]
                            det = sx * sy - 0.25 * (sxy * sxy)
                            root = lax.rsqrt(det)
                            chi = dy * (sxy * dx - sx * dy) - sy * (dx * dx)
                            like = jnp.exp2(chi * (root * root)) * root
                            like = jnp.where(step <= 2, like, 0.0)
                            acc[g][0] = acc[g][0] + like
                            if c == 0:
                                acc[g][1] = acc[g][1] + like * dx
                                acc[g][2] = acc[g][2] + like * dy
                    return tuple(tuple(a) for a in acc)

                zero = jnp.zeros((8, LANES), f32)
                acc = tuple((zero,) * (3 if c == 0 else 1) for _ in range(GROUPS))
                acc = lax.fori_loop(0, ends[other], pairs, acc)
                for g in range(GROUPS):
                    for k, a in enumerate(acc[g]):
                        totals[3 * c + k, pl.ds(base + 8 * g, 8), :] = a
                return 0

            lax.fori_loop(0, blocks, own_block, 0)

        f_of_lane = lane8 & (SLOT_LANES - 1)

        def sum_rows(first, last):
            for c in range(2):
                for g in range(first // 8, last // 8):
                    live = (iota((8, LANES), 0) + 8 * g) < count_own[c]
                    value = jnp.zeros((8, LANES), f32)
                    for k in range(3 if c == 0 else 1):
                        total = jnp.sum(totals[3 * c + k, 8 * g : 8 * g + 8, :], axis=1, keepdims=True) * GAIN
                        value = jnp.where(f_of_lane == c * FIELDS + k, total, value)
                    values[c * own_width + 8 * g : c * own_width + 8 * g + 8, :] = jnp.where(live, value, 0.0)

        many = jnp.maximum(count_own[0], count_own[1]) > early
        sum_rows(0, early)

        @pl.when(many)
        def _():
            sum_rows(early, own_width)

        @pl.when(jnp.logical_not(many))
        def _():
            for c in range(2):
                values[c * own_width + early : (c + 1) * own_width, :] = jnp.zeros((own_width - early, LANES), f32)

        result = sum(dot(pick[...], part, ((1,), (0,))) for part in split3(values[...])[:2])
        slot_of_lane = iota((peers, LANES), 1) >> 4
        final = jnp.zeros((peers, LANES), f32)
        for s in range(slots):
            final = final + jnp.where(slot_of_lane == s, result[s * peers : (s + 1) * peers, :], 0.0)
        out[...] = final

    return body


def return_body(sub_count, peers):
    slots = CAP * sub_count

    def body(back, places, like, offset, wise):
        n = places.shape[1]
        at = jnp.concatenate([places[0:1, :], places[1:2, :]], axis=1)
        rank_g, rank_w = places[2:3, :], places[3:4, :]
        pick = one_hot(iota((peers, 2 * n), 0) == at)
        turned = jnp.transpose(back[...])
        found = sum(dot(part, pick, ((1,), (0,))) for part in split3(turned)[:2])
        gaia = jnp.zeros((FIELDS, n), f32)
        other = jnp.zeros((FIELDS, n), f32)
        for s in range(slots):
            at = s * SLOT_LANES
            gaia = gaia + jnp.where(rank_g == s, found[at : at + FIELDS, 0:n], 0.0)
            other = other + jnp.where(rank_w == s, found[at + FIELDS : at + 2 * FIELDS, n : 2 * n], 0.0)
        like[...] = gaia[0:1, :]
        offset[...] = gaia[1:3, :]
        wise[...] = other[0:1, :]

    return body


def stages(pix_count, sub_count, rep_count, n):
    peers = pix_count
    members = sub_count * rep_count
    slots = CAP * sub_count
    width = 3 * peers * slots
    own_width = peers * slots
    rows = part_rows()
    parts = width // LANES // PART
    pair, line, whole = pltpu.VMEM((2, n), f32), pltpu.VMEM((1, n), f32), pltpu.VMEM((1, n), i32)
    send = call(
        send_body(pix_count, sub_count, peers),
        (jax.ShapeDtypeStruct((3 * peers, LANES), f32), jax.ShapeDtypeStruct((8, n), i32)),
    )
    compact = call(
        compact_body(peers, slots, members, width),
        (
            jax.ShapeDtypeStruct((members, rows, LANES), f32),
            jax.ShapeDtypeStruct(((parts - 1) * rows, LANES), f32),
            jax.ShapeDtypeStruct((2 * FIELDS, own_width), f32),
            jax.ShapeDtypeStruct((LANES, LANES), f32),
        ),
        [pltpu.VMEM((parts * rows, LANES), f32)],
    )
    results = jax.ShapeDtypeStruct((peers, LANES), f32)
    held = lambda tiles: [
        pltpu.VMEM((own_width + 8 * GROUPS, 2 * USED * LANES), f32),
        pltpu.VMEM((own_width, 2 * own_width), bf16),
        pltpu.VMEM((2, members * tiles + 8, FIELDS, LANES), f32),
        pltpu.VMEM((4, own_width + 8 * GROUPS, LANES), f32),
        pltpu.VMEM((2 * own_width, LANES), f32),
    ]
    match = call(
        match_body(peers, slots, members, PART),
        (results, jax.ShapeDtypeStruct((1, 1), i32)),
        held(PART),
        out_specs=(pl.BlockSpec(memory_space=pltpu.VMEM), pl.BlockSpec(memory_space=pltpu.SMEM)),
    )
    match_whole = call(match_body(peers, slots, members, width // LANES), results, held(width // LANES))
    back = call(
        return_body(sub_count, peers),
        (
            jax.ShapeDtypeStruct((1, n), f32),
            jax.ShapeDtypeStruct((2, n), f32),
            jax.ShapeDtypeStruct((1, n), f32),
        ),
    )
    return send, compact, match, match_whole, back


def shards(gaia_pos, gaia_shape, gaia_corr, gaia_dest, gaia_cell, wise_pos, wise_shape, wise_corr, wise_dest, wise_cell):
    pix_count = lax.axis_size("pix")
    sub_count = lax.axis_size("sub")
    rep_count = lax.axis_size("rep")
    peers = pix_count
    members = sub_count * rep_count
    n = gaia_pos.shape[1]
    send, compact, match, match_whole, back = stages(pix_count, sub_count, rep_count, n)
    row = lambda x: x.reshape(1, n)
    gd, wd = row(gaia_dest), row(wise_dest)
    msg, places = send(gaia_pos, gaia_shape, row(gaia_corr), gd, row(gaia_cell), wise_pos, wise_shape, row(wise_corr), wd, row(wise_cell))
    ring = [[(i + ring_start(pix_count)) % pix_count for i in range(pix_count)]]
    exchange = lambda x: lax.all_to_all(x, "pix", 0, 0, axis_index_groups=ring, tiled=True)
    got = exchange(msg.reshape(peers, 1, 3 * LANES))
    chunks, rest, own, ranks = compact(got.reshape(3 * peers, LANES))
    gather = lambda x: lax.all_to_all(x, ("sub", "rep"), 0, 0, tiled=True).reshape(-1, LANES)
    near = gather(chunks)
    results, over = match(near, own, ranks)

    def with_rest():
        return match_whole(near, gather(jnp.broadcast_to(rest[None], (members, *rest.shape))), own, ranks)

    results = lax.cond(over[0, 0] > 0, with_rest, lambda: results)
    returned = exchange(results.reshape(peers, 1, LANES))
    like, offset, wise = back(returned.reshape(peers, LANES), places)
    return like.reshape(n), offset, wise.reshape(n)


def solution(mesh):
    flat = P(("groups", "pix", "sub", "rep"))
    pair = P(None, ("groups", "pix", "sub", "rep"))
    column = P(("groups", "pix", "sub", "rep"), None)
    return jax.shard_map(
        shards,
        mesh=mesh,
        in_specs=(pair, pair, flat, column, flat, pair, pair, flat, column, flat),
        out_specs=(flat, pair, flat),
        check_vma=False,
    )
```

profile of v0, /device:TPU:40, one launch (start us, length us, event | category | flops | bytes accessed | tf_op | source)
XLA Modules:
  0.0 114.1 jit_solution(2077383942432674058)
XLA Ops:
  0.6 0.0 copy-start.7
  0.6 0.0 copy-start.8
  0.7 0.0 copy-start.9
  0.7 0.0 copy-start.3
  0.7 0.0 copy-start.5
  0.7 0.0 copy-start.6
  0.7 0.0 copy-start.1
  0.7 0.0 copy-start.2
  0.7 0.0 copy-start
  0.7 0.0 copy-start.4
  0.7 0.6 copy-done.7
  1.3 0.0 copy-done.8
  1.3 0.0 copy-done.9
  1.3 0.0 copy-done.3
  1.4 0.0 copy-done.5
  1.4 0.0 copy-done.6
  1.4 0.0 copy-done.1
  1.4 0.0 copy-done.2
  1.4 0.0 copy-done
  1.4 0.0 copy-done.4
  1.4 0.4 shard_map.121
  1.9 67.3 %all_to_all.20 = f32[32,1,384]{2,1,0:T(1,128)S(1)} all-to-all(f32[32,1,384]{2,1,0:T(1,128)S(1)} %bitcast.18), channel_id=1, replica_groups={{192,200,208,216,224,232,240,248,0,8,16,24,32,40,48,56,64,72,80,88,96,1..., dimensions={0} | all-to-all | bytes 98304 | tf_op jit(solution)/shard_map/all_to_all | solution.py:479
  69.1 1.4 %shard_map.122 = (f32[8,40,128]{2,1,0:T(8,128)S(1)}, f32[40,128]{1,0:T(8,128)S(1)}, f32[16,256]{1,0:T(8,128)S(1)}, f32[128,128]{1,0:T(8,128)S(1)}) custom-call(f32[96,128]{1,0:T(8,128)S(1)} %bitcast.16), custom_call_target="tpu_custom_call" | custom-call | tf_op jit(solution)/shard_map/pallas_call | solution.py:481
  70.6 10.8 %all_to_all.21 = f32[8,40,128]{2,1,0:T(8,128)S(1)} all-to-all(f32[8,40,128]{2,1,0:T(8,128)S(1)} %get-tuple-element.31), channel_id=1, replica_groups=mesh['groups'=2,'pix'=32,'sub'=4,'rep'=2] {'sub','rep'}, dimensions={0} | all-to-all | bytes 327680 | tf_op jit(solution)/shard_map/all_to_all | solution.py:482
  81.4 3.9 %shard_map.123 = (f32[32,128]{1,0:T(8,128)S(1)}, s32[1,1]{1,0:T(1,128)}) custom-call(f32[320,128]{1,0:T(8,128)S(1)} %bitcast.25, f32[16,256]{1,0:T(8,128)S(1)} %get-tuple-element.32.refs_1_, f32[128,128]{1,0:T(8,128)S(1)} %get-tuple-element.33.refs_2_), custom_call_target="tpu_custom_call" | custom-call | tf_op jit(solution)/shard_map/pallas_call | solution.py:484
  85.9 27.4 %all_to_all.22 = f32[32,1,128]{2,1,0:T(1,128)S(1)} all-to-all(f32[32,1,128]{2,1,0:T(1,128)S(1)} %bitcast.27), channel_id=1, replica_groups={{192,200,208,216,224,232,240,248,0,8,16,24,32,40,48,56,64,72,80,88,96,1..., dimensions={0} | all-to-all | bytes 32768 | tf_op jit(solution)/shard_map/all_to_all | solution.py:479
  113.3 0.8 shard_map.124
  (1 shorter events, 0.0 us)
Async XLA Ops:
  0.6 0.7 copy-start.7
  0.6 0.7 copy-start.8
  0.7 0.7 copy-start.9
  0.7 0.7 copy-start.3
  0.7 0.7 copy-start.5
  0.7 0.7 copy-start.6
  0.7 0.7 copy-start.1
  0.7 0.7 copy-start.2
  0.7 0.7 copy-start
  0.7 0.7 copy-start.4
where the time goes:
time: 114 us
  blocking collectives  105 us (92%)
  Pallas kernels  6.5 us (6%)
  between operations  1.39 us (1%)
    all_to_all x2, blocking collectives, shards(): lax.all_to_all(x, 'pix', 0, 0, axis_index_groups=ring, tiled=True)  94.6 us
    all_to_all x1, blocking collectives, shards(): lax.all_to_all(x, ('sub', 'rep'), 0, 0, tiled=True).reshape(-1, LANES)  10.8 us
    pallas_call x1, Pallas kernels, shards(): results, over = match(near, own, ranks)  3.87 us

commit v1 on v0

--- a/solution.py
+++ b/solution.py
@@ -58,7 +58,7 @@
 
 
 def ring_start(pix_count):
-    return pix_count * 3 // 4
+    return pix_count * 5 // 8
 
 
 def part_rows():
@@ -230,8 +230,7 @@
         spread_to = iota((6 * FIELDS, used * LANES), 1) >> 7
         field_of = spread_to + jnp.where(spread_to >= USED, FIELDS - USED, 0)
         spread = one_hot((iota((6 * FIELDS, used * LANES), 0) & (2 * FIELDS - 1)) == field_of)
-        wide[0:own_width, :] = dot(columns, spread, ((1,), (0,)))
-        wide[own_width:, :] = jnp.zeros((8 * GROUPS, used * LANES), f32)
+        wide[...] = dot(columns, spread, ((1,), (0,)))
         goal = iota((peers, own_width), 1).astype(f32)
         for c in range(2):
             for s in range(slots):
@@ -440,10 +439,10 @@
     )
     results = jax.ShapeDtypeStruct((peers, LANES), f32)
     held = lambda tiles: [
-        pltpu.VMEM((own_width + 8 * GROUPS, 2 * USED * LANES), f32),
+        pltpu.VMEM((own_width, 2 * USED * LANES), f32),
         pltpu.VMEM((own_width, 2 * own_width), bf16),
         pltpu.VMEM((2, members * tiles + 8, FIELDS, LANES), f32),
-        pltpu.VMEM((4, own_width + 8 * GROUPS, LANES), f32),
+        pltpu.VMEM((4, own_width, LANES), f32),
         pltpu.VMEM((2 * own_width, LANES), f32),
     ]
     match = call(
@@ -479,7 +478,7 @@
     exchange = lambda x: lax.all_to_all(x, "pix", 0, 0, axis_index_groups=ring, tiled=True)
     got = exchange(msg.reshape(peers, 1, 3 * LANES))
     chunks, rest, own, ranks = compact(got.reshape(3 * peers, LANES))
-    gather = lambda x: lax.all_to_all(x, ("sub", "rep"), 0, 0, tiled=True).reshape(-1, LANES)
+    gather = lambda x: lax.all_to_all(x, ("rep", "sub"), 0, 0, tiled=True).reshape(-1, LANES)
     near = gather(chunks)
     results, over = match(near, own, ranks)
 

time: 114 us -> 113 us (level)
  no operation moved by 1% of the time
where the time goes in v1:
time: 113 us; the launch traced here: 114 us
  blocking collectives  106 us (94%)
  Pallas kernels  5.96 us (5%)
  between operations  1.39 us (1%)
    all_to_all x2, blocking collectives, shards(): lax.all_to_all(x, 'pix', 0, 0, axis_index_groups=ring, tiled=True)  95.5 us
    all_to_all x1, blocking collectives, shards(): lax.all_to_all(x, ('rep', 'sub'), 0, 0, tiled=True).reshape(-1, LANES)  10.1 us
    pallas_call x1, Pallas kernels, shards(): results, over = match(near, own, ranks)  3.34 us

profile of v1, /device:TPU:40, one launch (start us, length us, event | category | flops | bytes accessed | tf_op | source)
XLA Modules:
  0.0 113.7 jit_solution(4993403884620723373)
XLA Ops:
  0.6 0.0 copy-start.7
  0.6 0.0 copy-start.8
  0.7 0.0 copy-start.9
  0.7 0.0 copy-start.3
  0.7 0.0 copy-start.5
  0.7 0.0 copy-start.6
  0.7 0.0 copy-start.1
  0.7 0.0 copy-start.2
  0.7 0.0 copy-start
  0.7 0.0 copy-start.4
  0.7 0.6 copy-done.7
  1.3 0.0 copy-done.8
  1.3 0.0 copy-done.9
  1.3 0.0 copy-done.3
  1.4 0.0 copy-done.5
  1.4 0.0 copy-done.6
  1.4 0.0 copy-done.1
  1.4 0.0 copy-done.2
  1.4 0.0 copy-done
  1.4 0.0 copy-done.4
  1.4 0.4 shard_map.121
  1.9 67.3 %all_to_all.20 = f32[32,1,384]{2,1,0:T(1,128)S(1)} all-to-all(f32[32,1,384]{2,1,0:T(1,128)S(1)} %bitcast.18), channel_id=1, replica_groups={{160,168,176,184,192,200,208,216,224,232,240,248,0,8,16,24,32,40,48,56,..., dimensions={0} | all-to-all | bytes 98304 | tf_op jit(solution)/shard_map/all_to_all | solution.py:478
  69.2 1.4 %shard_map.122 = (f32[8,40,128]{2,1,0:T(8,128)S(1)}, f32[40,128]{1,0:T(8,128)S(1)}, f32[16,256]{1,0:T(8,128)S(1)}, f32[128,128]{1,0:T(8,128)S(1)}) custom-call(f32[96,128]{1,0:T(8,128)S(1)} %bitcast.16), custom_call_target="tpu_custom_call" | custom-call | tf_op jit(solution)/shard_map/pallas_call | solution.py:480
  70.6 10.1 %all_to_all.21 = f32[8,40,128]{2,1,0:T(8,128)S(1)} all-to-all(f32[8,40,128]{2,1,0:T(8,128)S(1)} %get-tuple-element.31), channel_id=1, replica_groups=mesh['groups'=2,'pix'=32,'sub'=4,'rep'=2] {'rep','sub'}, dimensions={0} | all-to-all | bytes 327680 | tf_op jit(solution)/shard_map/all_to_all | solution.py:481
  80.7 3.3 %shard_map.123 = (f32[32,128]{1,0:T(8,128)S(1)}, s32[1,1]{1,0:T(1,128)}) custom-call(f32[320,128]{1,0:T(8,128)S(1)} %bitcast.25, f32[16,256]{1,0:T(8,128)S(1)} %get-tuple-element.32.refs_1_, f32[128,128]{1,0:T(8,128)S(1)} %get-tuple-element.33.refs_2_), custom_call_target="tpu_custom_call" | custom-call | tf_op jit(solution)/shard_map/pallas_call | solution.py:483
  84.7 28.3 %all_to_all.22 = f32[32,1,128]{2,1,0:T(1,128)S(1)} all-to-all(f32[32,1,128]{2,1,0:T(1,128)S(1)} %bitcast.27), channel_id=1, replica_groups={{160,168,176,184,192,200,208,216,224,232,240,248,0,8,16,24,32,40,48,56,..., dimensions={0} | all-to-all | bytes 32768 | tf_op jit(solution)/shard_map/all_to_all | solution.py:478
  112.9 0.8 shard_map.124
  (1 shorter events, 0.0 us)
Async XLA Ops:
  0.6 0.7 copy-start.7
  0.6 0.7 copy-start.8
  0.7 0.7 copy-start.9
  0.7 0.7 copy-start.3
  0.7 0.7 copy-start.5
  0.7 0.7 copy-start.6
  0.7 0.7 copy-start.1
  0.7 0.7 copy-start.2
  0.7 0.7 copy-start
  0.7 0.7 copy-start.4
